TPU v7x, 128 devices: a whole 4x4x4 slice. The times are simulated.
128 devices in a mesh: replica: 1, data2: 16 (over z, y), data: 8 (over x, core).
Axes of the slice: x: 4, y: 4, z: 4, core: 2. Of those that a mesh axis runs over, the one named last changes fastest.
Arguments:
- query_hidden: bfloat16 [512, 32, 768], P(('replica', 'data2', 'data'))
- doc_hidden: bfloat16 [512, 512, 768], P(('replica', 'data2', 'data'))
- w_proj: bfloat16 [768, 128], replicated
- query_mask: int32 [512, 32], P(('replica', 'data2', 'data'))
- doc_mask: int32 [512, 512], P(('replica', 'data2', 'data'))
- temperature: float32 [], replicated
Outputs:
- output 1: float32 [512], P(('replica', 'data2', 'data'))
- output 2: float32 [1], P('replica')
All inputs are finite; a program needn't handle non-finite values.
Results may differ from a plain program's by a relative error of at most 0.001.
Values are sent between devices in bfloat16 or wider.
A program may use at most 1 GiB of HBM per device.

v0:
```python
import jax
import jax.numpy as jnp
from jax import lax
from jax.sharding import PartitionSpec as P


def project_norm(hidden, w_proj):
    projected = jnp.einsum('bld,de->ble', hidden, w_proj, preferred_element_type=jnp.float32)
    norm_len = jnp.sqrt(jnp.sum(projected * projected, axis=-1, keepdims=True))
    return (projected / jnp.maximum(norm_len, 1e-12)).astype(jnp.bfloat16)


def tile_scores(q_block, p_block, doc_valid):
    similarity = jnp.einsum('qtc,jsc->qtjs', q_block, p_block, preferred_element_type=jnp.float32)
    best_match = jnp.max(jnp.where(doc_valid[None, None], similarity, -jnp.inf), axis=-1)
    return jnp.sum(best_match, axis=1)


def solution(mesh):
    outer_size = mesh.shape['data2']
    inner_size = mesh.shape['data']
    group_size = outer_size * inner_size
    batch_axes = ('data2', 'data')
    row_spec = P(('replica', 'data2', 'data'))
    tok_spec = P(('replica', 'data2', 'data'), None, None)
    mask_spec = P(('replica', 'data2', 'data'), None)

    def local_step(query_hidden, doc_hidden, w_proj, query_mask, doc_mask, value_a11):
        local_batch = query_hidden.shape[0]
        total_batch = local_batch * group_size
        q_vecs = project_norm(query_hidden, w_proj)
        q_vecs = jnp.where(query_mask[:, :, None] > 0, q_vecs, jnp.zeros_like(q_vecs))
        p_vecs = project_norm(doc_hidden, w_proj)
        doc_valid = doc_mask > 0
        q_all = lax.all_gather(q_vecs, 'data', axis=0, tiled=True)
        q_all = lax.all_gather(q_all, 'data2', axis=0, tiled=True)
        q_blocks = q_all.reshape(group_size, local_batch, q_all.shape[1], q_all.shape[2])
        column = lax.map(lambda q_block: tile_scores(q_block, p_vecs, doc_valid), q_blocks)
        column = column.reshape(outer_size, inner_size, local_batch, local_batch)
        column = lax.all_to_all(column, 'data', 1, 1, tiled=True)
        column = lax.all_to_all(column, 'data2', 0, 0, tiled=True)
        score_row = jnp.transpose(column, (2, 0, 1, 3)).reshape(local_batch, total_batch)
        logits = score_row / value_a11
        home_index = lax.axis_index('data2') * inner_size + lax.axis_index('data')
        own_logits = lax.dynamic_slice_in_dim(logits, home_index * local_batch, local_batch, axis=1)
        losses = jax.nn.logsumexp(logits, axis=1) - jnp.diagonal(own_logits)
        mean_loss = lax.psum(jnp.sum(losses), batch_axes) / total_batch
        return losses, mean_loss.reshape(1)

    return jax.shard_map(local_step, mesh=mesh, in_specs=(tok_spec, tok_spec, P(None, None), mask_spec, mask_spec, P()), out_specs=(row_spec, P('replica')), check_vma=False)
```

profile of v0, /device:TPU:1, one launch (start us, length us, event | category | flops | bytes accessed | tf_op | source)
XLA Modules:
  0.0 374.6 jit_solution(5241328455471896500)
XLA Ops:
  7.2 1.4 multiply_reduce_fusion.1
  9.5 14.5 %all_gather.6 = bf16[32,32,128]{2,1,0:T(8,128)(2,1)} all-gather(bf16[4,32,128]{2,1,0:T(8,128)(2,1)S(1)} %fusion.9), channel_id=1, replica_groups=mesh['replica'=1,'data2'=16,'data'=8] {'data'}, dimensions={0}, use_global_device_ids=true | all-gather | bytes 294912 | tf_op jit(solution)/shard_map/all_gather | solution.py:35
  24.0 2.1 multiply_reduce_fusion
  27.1 2.0 copy.18
  29.1 47.2 %all-gather.2.cloned.1.call-done = bf16[512,32,128]{2,1,0:T(8,128)(2,1)} async-done(((bf16[32,32,128]{2,1,0:T(8,128)(2,1)}), bf16[512,32,128]{2,1,0:T(8,128)(2,1)}) %all-gather.2.cloned.1.call-update) | async-done | bytes 4194320 | tf_op jit(solution)/shard_map/all_gather | solution.py:36
  76.4 198.5 %while.10 = (s32[]{:T(128)}, f32[128,4,4]{2,1,0:T(4,128)S(1)}, pred[4,512]{1,0:T(4,128)(4,1)S(1)}, bf16[128,4,32,128]{3,2,1,0:T(8,128)(2,1)}, bf16[4,512,128]{2,1,0:T(8,128)(2,1)}, /*index=5*/s32[]{:T(128)}, f32[]{:T(128)}) while((s32[]{:T(128)}, f32[128,4,4]{2,1,0:T(4,128)S(1)}, pred[4,512]{1,0:T(4,128)(4,1)S(1)}, ...), condition=%wide.region_5.6_spmd, body=%wide.region_2.5_spmd.sunk | while | flops 67633136 | bytes 567957 | solution.py:38
  81.0 1.4 fusion.19
  82.6 1.4 fusion.19
  84.1 1.4 fusion.19
  88.8 1.4 fusion.19
  90.4 1.4 fusion.19
  99.7 1.4 fusion.19
  113.6 1.4 fusion.19
  115.2 1.4 fusion.19
  127.6 1.4 fusion.19
  129.1 1.4 fusion.19
  143.1 1.4 fusion.19
  247.0 1.4 fusion.19
  261.0 1.4 fusion.19
  262.5 1.4 fusion.19
  275.3 9.8 %all_to_all.10 = f32[8,1,256]{2,1,0:T(1,128)S(1)} all-to-all(f32[8,1,256]{2,1,0:T(1,128)S(1)} %reshape.53), channel_id=1, replica_groups=mesh['replica'=1,'data2'=16,'data'=8] {'data'}, dimensions={0} | all-to-all | bytes 16384 | tf_op jit(solution)/shard_map/all_to_all | solution.py:40
  287.3 4.8 %all-to-all-start.1 = ((f32[16,1,128]{2,1,0:T(1,128)}), f32[16,1,128]{2,1,0:T(1,128)S(1)}, u32[]{:S(2)}, u32[]{:S(2)}) async-start(f32[16,1,128]{2,1,0:T(1,128)} %reshape.55), calls=%async_computation.1 | async-start | bytes 16384 | tf_op jit(solution)/shard_map/all_to_all | solution.py:41
  292.8 5.6 %all-to-all-done.1 = f32[16,1,128]{2,1,0:T(1,128)S(1)} async-done(((f32[16,1,128]{2,1,0:T(1,128)}), f32[16,1,128]{2,1,0:T(1,128)S(1)}, u32[]{:S(2)}, u32[]{:S(2)}) %all-to-all-start.1) | async-done | bytes 8224 | tf_op jit(solution)/shard_map/all_to_all | solution.py:41
  302.1 63.9 %psum.7 = f32[]{:T(128)} all-reduce(f32[]{:T(128)} %get-tuple-element.60), channel_id=1, replica_groups=mesh['replica'=1,'data2'=16,'data'=8] {'data2','data'}, use_global_device_ids=true, to_apply=%region_9.10 | all-reduce | flops 1 | bytes 8 | tf_op jit(solution)/shard_map/psum | solution.py:47
  (401 shorter events, 185.6 us)
Async XLA Ops:
  7.2 16.8 %copy-start = (bf16[4,512,768]{2,1,0:T(8,128)(2,1)S(1)}, bf16[4,512,768]{2,1,0:T(8,128)(2,1)}, u32[]{:S(2)}) copy-start(bf16[4,512,768]{2,1,0:T(8,128)(2,1)} %param.9) | copy-start | bytes 9437188
  7.2 69.2 %all-gather.2.cloned.1.call-start = ((), (), s32[]{:S(2)}) async-start(), calls=%async_computation.2 | async-start | bytes 4456448 | tf_op jit(solution)/shard_map/all_gather | solution.py:36
  24.0 5.1 %copy-start.1 = (s32[4,512]{1,0:T(4,128)S(1)}, s32[4,512]{1,0:T(4,128)}, u32[]{:S(2)}) copy-start(s32[4,512]{1,0:T(4,128)} %param.12) | copy-start | bytes 24580
  287.3 11.1 %all-to-all-start.1 = ((f32[16,1,128]{2,1,0:T(1,128)}), f32[16,1,128]{2,1,0:T(1,128)S(1)}, u32[]{:S(2)}, u32[]{:S(2)}) async-start(f32[16,1,128]{2,1,0:T(1,128)} %reshape.55), calls=%async_computation.1 | async-start | bytes 16384 | tf_op jit(solution)/shard_map/all_to_all | solution.py:41
Sparse Core Ops, SparseCore 0:
  24.1 52.2 all-gather.1
where the time goes:
time: 378 us; the launch traced here: 375 us
  matrix products  189 us (50%)
  blocking collectives  88.1 us (23%)
  waiting for transfers between devices  52.8 us (14%)
  between operations  16.6 us (4%)
  other arithmetic  15.8 us (4%)
  local copies, waits for them, and re-layouts  6.9 us (2%)
  starting transfers between devices  4.85 us (1%)
    dot_general x128, matrix products, tile_scores(): jnp.einsum('qtc,jsc->qtjs', q_block, p_block, preferred_element_type=jnp....  185 us
    psum x1, blocking collectives, local_step(): mean_loss = lax.psum(jnp.sum(losses), batch_axes) / total_batch  63.9 us
    all_gather x1, waiting for transfers between devices, local_step(): q_all = lax.all_gather(q_all, 'data2', axis=0, tiled=True)  47.2 us
    all_gather x1, blocking collectives, local_step(): q_all = lax.all_gather(q_vecs, 'data', axis=0, tiled=True)  14.5 us
    reduce_sum x128, other arithmetic, tile_scores(): return jnp.sum(best_match, axis=1)  11.3 us
    all_to_all x1, blocking collectives, local_step(): column = lax.all_to_all(column, 'data', 1, 1, tiled=True)  9.8 us
  transfers between devices with their start and end apart: 2, of which 2 were waited for; matrix products, arithmetic and copies ran while one was open for 1% of the time, Pallas kernels for 0%

commit v1 on v0

v1 whole, which is shorter than its diff:
```python
import jax
import jax.numpy as jnp
from jax import lax
from jax.experimental import pallas as pl
from jax.experimental.pallas import tpu as pltpu
from jax.sharding import PartitionSpec as P

MESH = pl.DeviceIdType.MESH
NQ, LQ, LD, HID, DIM = 4, 32, 512, 768, 128
SIDE = 4
TOTAL = 512
ORDERS = (('x', 'y', 'z'), ('y', 'z', 'x'), ('z', 'x', 'y'), ('x', 'z', 'y'))


def unit_rows(projected):
    square = jnp.sum(projected * projected, axis=-1, keepdims=True)
    return projected * jnp.minimum(lax.rsqrt(square), 1e12)


def kernel(qh_hbm, dh_hbm, w_hbm, qm_hbm, dm_hbm, temp_hbm, loss_ref, mean_ref,
           qh, dh, w, qm, dm, temp, qbuf, pbuf, sacc, xbuf, ybuf, zbuf,
           in_sem, send_sem, recv_sem):
    outer, inner = lax.axis_index('data2'), lax.axis_index('data')
    here = {'z': outer // SIDE, 'y': outer % SIDE, 'x': inner // 2}
    core = inner % 2

    def moved(axis, step, same_core=True):
        at = dict(here)
        at[axis] = (here[axis] + step) % SIDE
        c = core if same_core else 1 - core
        return {'data2': at['z'] * SIDE + at['y'], 'data': at['x'] * 2 + c}

    sibling = moved('x', 0, False)
    used = [0]
    sent = []

    def message():
        used[0] += 1
        return used[0] - 1

    def push(slot, src, dst, device):
        copy = pltpu.make_async_remote_copy(src_ref=src, dst_ref=dst, send_sem=send_sem.at[slot],
                                            recv_sem=recv_sem.at[slot], device_id=device, device_id_type=MESH)
        copy.start()
        sent.append(copy)

    def arrived(slot, dst):
        pltpu.make_async_remote_copy(src_ref=dst, dst_ref=dst, send_sem=send_sem.at[slot],
                                     recv_sem=recv_sem.at[slot], device_id=sibling, device_id_type=MESH).wait_recv()

    loads = [pltpu.make_async_copy(s, d, in_sem.at[i]) for i, (s, d) in enumerate(
        [(w_hbm, w), (qh_hbm, qh), (qm_hbm, qm), (dm_hbm, dm), (temp_hbm, temp)]
        + [(dh_hbm.at[d], dh.at[d]) for d in range(NQ)])]
    for load in loads:
        load.start()

    partners = [moved(a, s) for a in ('x', 'y', 'z') for s in (1, 2, 3)] + [moved('z', s, False) for s in range(SIDE)]
    barrier = pltpu.get_barrier_semaphore()
    for device in partners:
        pl.semaphore_signal(barrier, inc=1, device_id=device, device_id_type=MESH)

    def coords(o):
        return [here[a] for a in ORDERS[o]]

    def row_of(o, r3, r2):
        c1, c2, c3 = coords(o)
        return ((c3 + r3) % SIDE) * SIDE + (c2 + r2) % SIDE

    def row(o, r3, r2):
        return qbuf.at[o, row_of(o, r3, r2)]

    def block(o, r1):
        c1 = coords(o)[0]
        start = pl.multiple_of(((c1 + r1) % SIDE) * LQ, LQ)
        return qbuf.at[o, row_of(o, 0, 0), pl.ds(start, LQ)]

    loads[0].wait()
    loads[1].wait()
    loads[2].wait()
    mask_t = jnp.transpose(jnp.concatenate(
        [jnp.concatenate([qm[...].astype(jnp.float32), jnp.zeros((NQ, DIM - LQ), jnp.float32)], axis=1),
         jnp.zeros((8 - NQ, DIM), jnp.float32)], axis=0))
    for o in range(NQ):
        q = unit_rows(jnp.dot(qh[pl.ds(o * LQ, LQ)], w[...], preferred_element_type=jnp.float32))
        keep = mask_t[:LQ, o:o + 1] > 0
        block(o, 0)[...] = jnp.where(keep, q, 0.0).astype(jnp.bfloat16)
    sacc[...] = jnp.zeros_like(sacc)

    pl.semaphore_wait(barrier, len(partners))

    m1 = {(o, s): message() for o in range(NQ) for s in (1, 2, 3)}
    m2 = {(o, s): message() for o in range(NQ) for s in (1, 2, 3)}
    m3 = {(o, s, r): message() for o in range(NQ) for s in (1, 3) for r in range(SIDE)}
    m4 = {(o, r): message() for o in range(NQ) for r in range(SIDE)}
    mp = [message() for _ in range(NQ)]
    mx = {s: message() for s in (1, 2, 3)}
    my = {s: message() for s in (1, 2, 3)}
    mz = {(s, same): message() for s in range(SIDE) for same in (True, False) if s or not same}

    for s in (1, 3, 2):
        for o in range(NQ):
            push(m1[o, s], block(o, 0), block(o, 0), moved(ORDERS[o][0], s))

    loads[3].wait()
    valid = dm[...].astype(jnp.float32)
    key = valid * (LD - lax.broadcasted_iota(jnp.int32, (NQ, LD), 1)).astype(jnp.float32)
    key_t = jnp.transpose(jnp.concatenate([key, jnp.zeros((8 - NQ, LD), jnp.float32)], axis=0))
    for d in range(NQ):
        loads[5 + d].wait()
        p = unit_rows(jnp.dot(dh[d], w[...], preferred_element_type=jnp.float32))
        col = key_t[:, d:d + 1]
        first = jnp.max(col, axis=0, keepdims=True)
        colb = jnp.broadcast_to(col, (LD, DIM))
        stand_in = jnp.sum(jnp.where(colb == first, p, 0.0), axis=0, keepdims=True)
        pbuf[d] = jnp.where(colb > 0, p, stand_in).astype(jnp.bfloat16)
        push(mp[d], pbuf.at[d], pbuf.at[NQ + d], sibling)

    lane = lax.broadcasted_iota(jnp.int32, (8, DIM), 1)

    def score(units):
        for u, v in zip(units[::2], units[1::2]):
            q = jnp.concatenate([row(*u)[...], row(*v)[...]], axis=0)
            best = []
            for d in range(2 * NQ):
                sim = lax.dot_general(pbuf[d], q, (((1,), (1,)), ((), ())), preferred_element_type=jnp.float32)
                peak = jnp.max(sim.reshape(LD // 8, 8, 2 * DIM), axis=0)
                best.append(jnp.max(peak, axis=0, keepdims=True))
            best = jnp.concatenate(best, axis=0)
            for i, (o, r3, r2) in enumerate((u, v)):
                t = best[:, i * DIM:(i + 1) * DIM]
                for shift in (16, 8, 4, 2, 1):
                    t = t + pltpu.roll(t, DIM - shift, 1)
                place = (o % 2) * 16 + row_of(o, r3, r2)
                t = pltpu.roll(t, place, 1)
                sacc[o // 2] = jnp.where(lane % LQ == place, t, sacc[o // 2])

    def rows(*which):
        return [(o, r3, r2) for r3, r2 in which for o in range(NQ)]

    for o in range(NQ):
        for s in (1, 3, 2):
            arrived(m1[o, s], block(o, -s))
        for s in (1, 3, 2):
            push(m2[o, s], row(o, 0, 0), row(o, 0, 0), moved(ORDERS[o][1], s))
        for s in (1, 3):
            push(m3[o, s, 0], row(o, 0, 0), row(o, 0, 0), moved(ORDERS[o][2], s))
    for d in range(NQ):
        arrived(mp[d], pbuf.at[NQ + d])
    score(rows((0, 0)))

    def second(o, s):
        r = -s % SIDE
        arrived(m2[o, s], row(o, 0, r))
        for t in (1, 3):
            push(m3[o, t, r], row(o, 0, r), row(o, 0, r), moved(ORDERS[o][2], t))

    def third(o, s, r, forward):
        arrived(m3[o, s, r], row(o, -s, r))
        if forward:
            push(m4[o, r], row(o, -s, r), row(o, -s, r), moved(ORDERS[o][2], s))

    for o in range(NQ):
        second(o, 1)
        second(o, 3)
    score(rows((0, 1), (0, 3)))
    for o in range(NQ):
        second(o, 2)
    for o in range(NQ):
        third(o, 1, 0, True)
        third(o, 3, 0, False)
    score(rows((1, 0), (3, 0)))
    for o in range(NQ):
        third(o, 1, 1, True)
        third(o, 3, 3, True)
    for o in range(NQ):
        third(o, 1, 3, False)
        third(o, 3, 1, False)
    score(rows((0, 2), (1, 1)))
    for o in range(NQ):
        third(o, 3, 2, True)
        third(o, 1, 2, False)
    score(rows((1, 3), (3, 1)))
    score(rows((3, 3), (1, 2)))
    for o in range(NQ):
        arrived(m4[o, 0], row(o, 2, 0))
    score(rows((3, 2), (2, 0)))
    for o in range(NQ):
        arrived(m4[o, 1], row(o, 2, 1))
        arrived(m4[o, 3], row(o, 2, 3))
    score(rows((2, 1), (2, 3)))
    for o in range(NQ):
        arrived(m4[o, 2], row(o, 2, 2))
    score(rows((2, 2)))

    loads[4].wait()
    lane1 = lane[:1]
    sub = lax.broadcasted_iota(jnp.int32, (8, DIM), 0)

    def own_lane(o):
        c1, c2, c3 = coords(o)
        return c1 * LQ + (o % 2) * 16 + c3 * SIDE + c2

    tops, sums, positives = [], [], []
    for g in range(2):
        logit = sacc[g] / temp[0]
        top = jnp.max(logit, axis=0, keepdims=True)
        tops.append(top)
        sums.append(jnp.sum(jnp.exp(logit - top), axis=0, keepdims=True))
        mine = jnp.zeros((8, DIM), jnp.float32)
        for o in (2 * g, 2 * g + 1):
            mine = jnp.where((sub == o) & (lane == own_lane(o)), logit, mine)
        positives.append(jnp.sum(mine, axis=0, keepdims=True))
    part = jnp.concatenate(tops + sums + positives + [jnp.zeros((2, DIM), jnp.float32)], axis=0)

    def merge(parts):
        top = jnp.maximum(jnp.maximum(parts[0][0:2], parts[1][0:2]), jnp.maximum(parts[2][0:2], parts[3][0:2]))
        total = sum(p[2:4] * jnp.exp(p[0:2] - top) for p in parts)
        positive = sum(p[4:6] for p in parts)
        return top, total, positive

    def packed(top, total, positive):
        return jnp.concatenate([top, total, positive, jnp.zeros((2, DIM), jnp.float32)], axis=0)

    for axis, buf, slots in (('x', xbuf, mx), ('y', ybuf, my)):
        at = here[axis]
        buf[at] = part
        for s in (2, 1, 3):
            push(slots[s], buf.at[at], buf.at[at], moved(axis, s))
        for s in (1, 3, 2):
            arrived(slots[s], buf.at[(at - s) % SIDE])
        part = packed(*merge([buf[i] for i in range(SIDE)]))
    at = here['z']
    zbuf[core * SIDE + at] = part
    for s in (2, 1, 3, 0):
        for same in (True, False):
            if s or not same:
                push(mz[s, same], zbuf.at[core * SIDE + at], zbuf.at[core * SIDE + at], moved('z', s, same))
    for s in (0, 1, 3, 2):
        for same in (True, False):
            if s or not same:
                other = core if same else 1 - core
                arrived(mz[s, same], zbuf.at[other * SIDE + (at - s) % SIDE])
    total_loss = jnp.zeros((1, 1), jnp.float32)
    for c in range(2):
        top, total, positive = merge([zbuf[c * SIDE + i] for i in range(SIDE)])
        loss = top + jnp.log(total) - positive
        total_loss = total_loss + jnp.sum(jnp.sum(loss, axis=0, keepdims=True), axis=1, keepdims=True)
        if c == 0:
            losses = loss
        else:
            losses = jnp.where(core == 0, losses, loss)
    mean_ref[...] = total_loss / TOTAL
    row_loss = jnp.zeros((1, DIM), jnp.float32)
    for o in range(NQ):
        g = o // 2
        value = jnp.sum(jnp.where(lane1 == own_lane(o), losses[g:g + 1], 0.0), axis=1, keepdims=True)
        row_loss = jnp.where(lane1 == o, value, row_loss)
    loss_ref[...] = row_loss[:, :NQ]

    for copy in sent:
        copy.wait_send()


def solution(mesh):
    row_spec = P(('replica', 'data2', 'data'))
    tok_spec = P(('replica', 'data2', 'data'), None, None)
    mask_spec = P(('replica', 'data2', 'data'), None)
    n_msg = 12 + 12 + 32 + 16 + 4 + 3 + 3 + 7

    def local_step(query_hidden, doc_hidden, w_proj, query_mask, doc_mask, temperature):
        losses, mean = pl.pallas_call(
            kernel,
            out_shape=(jax.ShapeDtypeStruct((1, NQ), jnp.float32), jax.ShapeDtypeStruct((1, 1), jnp.float32)),
            in_specs=[pl.BlockSpec(memory_space=pl.ANY)] * 6,
            out_specs=(pl.BlockSpec(memory_space=pltpu.VMEM), pl.BlockSpec(memory_space=pltpu.VMEM)),
            scratch_shapes=[
                pltpu.VMEM((NQ * LQ, HID), jnp.bfloat16),
                pltpu.VMEM((NQ, LD, HID), jnp.bfloat16),
                pltpu.VMEM((HID, DIM), jnp.bfloat16),
                pltpu.VMEM((NQ, LQ), jnp.int32),
                pltpu.VMEM((NQ, LD), jnp.int32),
                pltpu.SMEM((1,), jnp.float32),
                pltpu.VMEM((NQ, SIDE * SIDE, SIDE * LQ, DIM), jnp.bfloat16),
                pltpu.VMEM((2 * NQ, LD, DIM), jnp.bfloat16),
                pltpu.VMEM((2, 8, DIM), jnp.float32),
                pltpu.VMEM((SIDE, 8, DIM), jnp.float32),
                pltpu.VMEM((SIDE, 8, DIM), jnp.float32),
                pltpu.VMEM((2 * SIDE, 8, DIM), jnp.float32),
                pltpu.SemaphoreType.DMA((9,)),
                pltpu.SemaphoreType.DMA((n_msg,)),
                pltpu.SemaphoreType.DMA((n_msg,)),
            ],
            compiler_params=pltpu.CompilerParams(collective_id=0, has_side_effects=True, vmem_limit_bytes=48 << 20),
            name='late_interaction_loss',
        )(query_hidden.reshape(NQ * LQ, HID), doc_hidden, w_proj, query_mask, doc_mask, temperature.reshape(1))
        return losses.reshape(NQ), mean.reshape(1)

    return jax.shard_map(local_step, mesh=mesh, in_specs=(tok_spec, tok_spec, P(None, None), mask_spec, mask_spec, P()),
                         out_specs=(row_spec, P('replica')), check_vma=False)
```

time: 378 us -> 59.3 us (0.16)
  matrix products: 189 us -> 0 us
  blocking collectives: 88.1 us -> 0 us
  waiting for transfers between devices: 52.8 us -> 0 us
  Pallas kernels: 0 us -> 50.4 us
  other arithmetic: 15.8 us -> 0 us
  between operations: 16.6 us -> 2.99 us
  starting transfers between devices: 4.85 us -> 0 us
    dot_general x130 -> x0, matrix products: 189 us -> none  [the longest x128 185 us: tile_scores(): jnp.einsum('qtc,jsc->qtjs', q_block, p_block, preferred_element_type=jnp....]
    psum x1 -> x0, blocking collectives: 63.9 us -> none  [local_step(): mean_loss = lax.psum(jnp.sum(losses), batch_axes) / total_batch]
    pallas_call x0 -> x1, Pallas kernels: none -> 50.4 us  [local_step(): pl.pallas_call(kernel, out_shape=(jax.ShapeDtypeStruct((1, NQ), jnp.float...]
    all_gather x1 -> x0, waiting for transfers between devices: 47.2 us -> none  [local_step(): q_all = lax.all_gather(q_all, 'data2', axis=0, tiled=True)]
    all_gather x1 -> x0, blocking collectives: 14.5 us -> none  [local_step(): q_all = lax.all_gather(q_vecs, 'data', axis=0, tiled=True)]
    reduce_sum x130 -> x0, other arithmetic: 12.6 us -> none  [the longest x128 11.3 us: tile_scores(): return jnp.sum(best_match, axis=1)]
    all_to_all x1 -> x0, blocking collectives: 9.8 us -> none  [local_step(): column = lax.all_to_all(column, 'data', 1, 1, tiled=True)]
    all_to_all x1 -> x0, waiting for transfers between devices: 5.56 us -> none  [local_step(): column = lax.all_to_all(column, 'data2', 0, 0, tiled=True)]
  transfers between devices with their start and end apart: 2 -> 0, of which waited for: 2 -> 0; matrix products, arithmetic and copies ran while one was open for 1% -> 0% of each run, Pallas kernels for 0% -> 0%
where the time goes in v1:
time: 59.3 us; the launch traced here: 59.1 us
  Pallas kernels  50.4 us (85%)
  local copies, waits for them, and re-layouts  5.63 us (9%)
  between operations  2.99 us (5%)
    pallas_call x1, Pallas kernels, local_step(): pl.pallas_call(kernel, out_shape=(jax.ShapeDtypeStruct((1, NQ), jnp.float...  50.4 us
    unnamed x11, local copies, waits for them, and re-layouts  5.63 us

profile of v1, /device:TPU:1, one launch (start us, length us, event | category | flops | bytes accessed | tf_op | source)
XLA Modules:
  0.0 59.1 jit_solution(6934382741811589488)
XLA Ops:
  1.3 0.0 copy-start
  1.3 1.9 %copy-done = bf16[4,512,768]{2,1,0:T(8,128)(2,1)S(1)} copy-done((bf16[4,512,768]{2,1,0:T(8,128)(2,1)S(1)}, bf16[4,512,768]{2,1,0:T(8,128)(2,1)}, u32[]{:S(2)}) %copy-start) | copy-done | bytes 3145752
  3.2 0.0 copy-start.1
  3.2 0.9 %copy-done.1 = bf16[4,32,768]{2,1,0:T(8,128)(2,1)S(1)} copy-done((bf16[4,32,768]{2,1,0:T(8,128)(2,1)S(1)}, bf16[4,32,768]{2,1,0:T(8,128)(2,1)}, u32[]{:S(2)}) %copy-start.1) | copy-done | bytes 196632
  4.1 0.0 copy-start.2
  4.1 0.9 %copy-done.2 = bf16[768,128]{1,0:T(8,128)(2,1)S(1)} copy-done((bf16[768,128]{1,0:T(8,128)(2,1)S(1)}, bf16[768,128]{1,0:T(8,128)(2,1)}, u32[]{:S(2)}) %copy-start.2) | copy-done | bytes 196632
  5.0 0.0 copy-start.3
  5.0 0.7 %copy-done.3 = s32[4,512]{1,0:T(4,128)S(1)} copy-done((s32[4,512]{1,0:T(4,128)S(1)}, s32[4,512]{1,0:T(4,128)}, u32[]{:S(2)}) %copy-start.3) | copy-done | bytes 8216
  5.7 0.0 copy-start.4
  5.7 0.7 %copy-done.4 = s32[4,32]{1,0:T(4,128)S(1)} copy-done((s32[4,32]{1,0:T(4,128)S(1)}, s32[4,32]{1,0:T(4,128)}, u32[]{:S(2)}) %copy-start.4) | copy-done | bytes 536
  6.4 50.4 %late_interaction_loss.1 = (f32[1,4]{1,0:T(1,128)S(1)}, f32[1,1]{1,0:T(1,128)}) custom-call(bf16[128,768]{1,0:T(8,128)(2,1)S(1)} %bitcast.5, bf16[4,512,768]{2,1,0:T(8,128)(2,1)S(1)} %copy-done, bf16[768,128]{1,0:T(8,128)(2,1)S(1)} %copy-done.2, s32[4,32]{1,0:T(4,128)S(1)} %copy-done.4, s32[4,512]{1,0:T(4,128)S(1)} %copy-done.3, f32[1]{0:T(128)} %bitcast.4.temp_hbm), custom_call_target="tpu_custom_call" | custom-call | tf_op jit(solution)/shard_map/late_interaction_loss/pallas_call | solution.py:271
  56.9 0.5 copy.11
Async XLA Ops:
  1.3 1.9 %copy-start = (bf16[4,512,768]{2,1,0:T(8,128)(2,1)S(1)}, bf16[4,512,768]{2,1,0:T(8,128)(2,1)}, u32[]{:S(2)}) copy-start(bf16[4,512,768]{2,1,0:T(8,128)(2,1)} %dh_hbm.1) | copy-start | bytes 9437188
  3.2 0.9 %copy-start.1 = (bf16[4,32,768]{2,1,0:T(8,128)(2,1)S(1)}, bf16[4,32,768]{2,1,0:T(8,128)(2,1)}, u32[]{:S(2)}) copy-start(bf16[4,32,768]{2,1,0:T(8,128)(2,1)} %param.6) | copy-start | bytes 589828
  4.1 0.9 %copy-start.2 = (bf16[768,128]{1,0:T(8,128)(2,1)S(1)}, bf16[768,128]{1,0:T(8,128)(2,1)}, u32[]{:S(2)}) copy-start(bf16[768,128]{1,0:T(8,128)(2,1)} %w_hbm.1) | copy-start | bytes 589828
  5.0 0.7 %copy-start.3 = (s32[4,512]{1,0:T(4,128)S(1)}, s32[4,512]{1,0:T(4,128)}, u32[]{:S(2)}) copy-start(s32[4,512]{1,0:T(4,128)} %dm_hbm.1) | copy-start | bytes 24580
  5.7 0.7 %copy-start.4 = (s32[4,32]{1,0:T(4,128)S(1)}, s32[4,32]{1,0:T(4,128)}, u32[]{:S(2)}) copy-start(s32[4,32]{1,0:T(4,128)} %qm_hbm.1) | copy-start | bytes 1540

commit v2 on v1

--- a/solution.py
+++ b/solution.py
@@ -1,3 +1,5 @@
+import functools
+
 import jax
 import jax.numpy as jnp
 from jax import lax
@@ -17,16 +19,17 @@
     return projected * jnp.minimum(lax.rsqrt(square), 1e12)
 
 
-def kernel(qh_hbm, dh_hbm, w_hbm, qm_hbm, dm_hbm, temp_hbm, loss_ref, mean_ref,
-           qh, dh, w, qm, dm, temp, qbuf, pbuf, sacc, xbuf, ybuf, zbuf,
+def kernel(qh_hbm, dh_hbm, w_hbm, qm_hbm, dm_hbm, temp_hbm, out_ref,
+           qh, dh, w, qm, dm, temp, qbuf, pbuf, sacc, xybuf, zbuf,
            in_sem, send_sem, recv_sem):
     outer, inner = lax.axis_index('data2'), lax.axis_index('data')
     here = {'z': outer // SIDE, 'y': outer % SIDE, 'x': inner // 2}
     core = inner % 2
 
-    def moved(axis, step, same_core=True):
+    def moved(axis, step, same_core=True, axis2='x', step2=0):
         at = dict(here)
-        at[axis] = (here[axis] + step) % SIDE
+        at[axis] = (at[axis] + step) % SIDE
+        at[axis2] = (at[axis2] + step2) % SIDE
         c = core if same_core else 1 - core
         return {'data2': at['z'] * SIDE + at['y'], 'data': at['x'] * 2 + c}
 
@@ -80,39 +83,50 @@
     mask_t = jnp.transpose(jnp.concatenate(
         [jnp.concatenate([qm[...].astype(jnp.float32), jnp.zeros((NQ, DIM - LQ), jnp.float32)], axis=1),
          jnp.zeros((8 - NQ, DIM), jnp.float32)], axis=0))
-    for o in range(NQ):
-        q = unit_rows(jnp.dot(qh[pl.ds(o * LQ, LQ)], w[...], preferred_element_type=jnp.float32))
+    q = unit_rows(jnp.dot(qh[...], w[...], preferred_element_type=jnp.float32))
+    for o in range(NQ):
         keep = mask_t[:LQ, o:o + 1] > 0
-        block(o, 0)[...] = jnp.where(keep, q, 0.0).astype(jnp.bfloat16)
+        block(o, 0)[...] = jnp.where(keep, q[o * LQ:(o + 1) * LQ], 0.0).astype(jnp.bfloat16)
     sacc[...] = jnp.zeros_like(sacc)
-
-    pl.semaphore_wait(barrier, len(partners))
 
     m1 = {(o, s): message() for o in range(NQ) for s in (1, 2, 3)}
     m2 = {(o, s): message() for o in range(NQ) for s in (1, 2, 3)}
     m3 = {(o, s, r): message() for o in range(NQ) for s in (1, 3) for r in range(SIDE)}
     m4 = {(o, r): message() for o in range(NQ) for r in range(SIDE)}
     mp = [message() for _ in range(NQ)]
-    mx = {s: message() for s in (1, 2, 3)}
-    my = {s: message() for s in (1, 2, 3)}
+    mxy = {(sx, sy): message() for sx in range(SIDE) for sy in range(SIDE) if sx or sy}
     mz = {(s, same): message() for s in range(SIDE) for same in (True, False) if s or not same}
-
-    for s in (1, 3, 2):
-        for o in range(NQ):
-            push(m1[o, s], block(o, 0), block(o, 0), moved(ORDERS[o][0], s))
 
     loads[3].wait()
     valid = dm[...].astype(jnp.float32)
     key = valid * (LD - lax.broadcasted_iota(jnp.int32, (NQ, LD), 1)).astype(jnp.float32)
     key_t = jnp.transpose(jnp.concatenate([key, jnp.zeros((8 - NQ, LD), jnp.float32)], axis=0))
-    for d in range(NQ):
-        loads[5 + d].wait()
+
+    def project(docs):
+        for d in docs:
+            loads[5 + d].wait()
+        for d in docs:
+            project_one(d)
+
+    def project_one(d):
         p = unit_rows(jnp.dot(dh[d], w[...], preferred_element_type=jnp.float32))
         col = key_t[:, d:d + 1]
         first = jnp.max(col, axis=0, keepdims=True)
         colb = jnp.broadcast_to(col, (LD, DIM))
         stand_in = jnp.sum(jnp.where(colb == first, p, 0.0), axis=0, keepdims=True)
         pbuf[d] = jnp.where(colb > 0, p, stand_in).astype(jnp.bfloat16)
+
+    project((0, 1))
+    pl.semaphore_wait(barrier, len(partners))
+
+    for s in (1, 3, 2):
+        for o in range(NQ):
+            push(m1[o, s], block(o, 0), block(o, 0), moved(ORDERS[o][0], s))
+
+    for d in (0, 1):
+        push(mp[d], pbuf.at[d], pbuf.at[NQ + d], sibling)
+    project((2, 3))
+    for d in (2, 3):
         push(mp[d], pbuf.at[d], pbuf.at[NQ + d], sibling)
 
     lane = lax.broadcasted_iota(jnp.int32, (8, DIM), 1)
@@ -140,13 +154,16 @@
     for o in range(NQ):
         for s in (1, 3, 2):
             arrived(m1[o, s], block(o, -s))
-        for s in (1, 3, 2):
+        for s in (1, 3):
             push(m2[o, s], row(o, 0, 0), row(o, 0, 0), moved(ORDERS[o][1], s))
+    for o in range(NQ):
         for s in (1, 3):
             push(m3[o, s, 0], row(o, 0, 0), row(o, 0, 0), moved(ORDERS[o][2], s))
     for d in range(NQ):
         arrived(mp[d], pbuf.at[NQ + d])
     score(rows((0, 0)))
+    for o in range(NQ):
+        push(m2[o, 2], row(o, 0, 0), row(o, 0, 0), moved(ORDERS[o][1], 2))
 
     def second(o, s):
         r = -s % SIDE
@@ -164,10 +181,10 @@
         second(o, 3)
     score(rows((0, 1), (0, 3)))
     for o in range(NQ):
-        second(o, 2)
-    for o in range(NQ):
         third(o, 1, 0, True)
         third(o, 3, 0, False)
+    for o in range(NQ):
+        second(o, 2)
     score(rows((1, 0), (3, 0)))
     for o in range(NQ):
         third(o, 1, 1, True)
@@ -179,15 +196,12 @@
     for o in range(NQ):
         third(o, 3, 2, True)
         third(o, 1, 2, False)
-    score(rows((1, 3), (3, 1)))
-    score(rows((3, 3), (1, 2)))
+    score(rows((1, 3), (3, 1), (3, 3), (1, 2)))
     for o in range(NQ):
         arrived(m4[o, 0], row(o, 2, 0))
-    score(rows((3, 2), (2, 0)))
-    for o in range(NQ):
         arrived(m4[o, 1], row(o, 2, 1))
         arrived(m4[o, 3], row(o, 2, 3))
-    score(rows((2, 1), (2, 3)))
+    score(rows((3, 2), (2, 0), (2, 1), (2, 3)))
     for o in range(NQ):
         arrived(m4[o, 2], row(o, 2, 2))
     score(rows((2, 2)))
@@ -213,22 +227,19 @@
     part = jnp.concatenate(tops + sums + positives + [jnp.zeros((2, DIM), jnp.float32)], axis=0)
 
     def merge(parts):
-        top = jnp.maximum(jnp.maximum(parts[0][0:2], parts[1][0:2]), jnp.maximum(parts[2][0:2], parts[3][0:2]))
+        top = functools.reduce(jnp.maximum, [p[0:2] for p in parts])
         total = sum(p[2:4] * jnp.exp(p[0:2] - top) for p in parts)
         positive = sum(p[4:6] for p in parts)
         return top, total, positive
 
-    def packed(top, total, positive):
-        return jnp.concatenate([top, total, positive, jnp.zeros((2, DIM), jnp.float32)], axis=0)
-
-    for axis, buf, slots in (('x', xbuf, mx), ('y', ybuf, my)):
-        at = here[axis]
-        buf[at] = part
-        for s in (2, 1, 3):
-            push(slots[s], buf.at[at], buf.at[at], moved(axis, s))
-        for s in (1, 3, 2):
-            arrived(slots[s], buf.at[(at - s) % SIDE])
-        part = packed(*merge([buf[i] for i in range(SIDE)]))
+    at = here['y'] * SIDE + here['x']
+    xybuf[at] = part
+    plane = [(sx, sy) for sy in (2, 1, 3, 0) for sx in (2, 1, 3, 0) if sx or sy]
+    for sx, sy in plane:
+        push(mxy[sx, sy], xybuf.at[at], xybuf.at[at], moved('x', sx, True, 'y', sy))
+    for sx, sy in plane[::-1]:
+        arrived(mxy[sx, sy], xybuf.at[((here['y'] - sy) % SIDE) * SIDE + (here['x'] - sx) % SIDE])
+    part = jnp.concatenate([*merge([xybuf[i] for i in range(SIDE * SIDE)]), jnp.zeros((2, DIM), jnp.float32)], axis=0)
     at = here['z']
     zbuf[core * SIDE + at] = part
     for s in (2, 1, 3, 0):
@@ -249,30 +260,34 @@
             losses = loss
         else:
             losses = jnp.where(core == 0, losses, loss)
-    mean_ref[...] = total_loss / TOTAL
     row_loss = jnp.zeros((1, DIM), jnp.float32)
     for o in range(NQ):
         g = o // 2
         value = jnp.sum(jnp.where(lane1 == own_lane(o), losses[g:g + 1], 0.0), axis=1, keepdims=True)
         row_loss = jnp.where(lane1 == o, value, row_loss)
-    loss_ref[...] = row_loss[:, :NQ]
+    out_ref[...] = jnp.concatenate([row_loss, jnp.broadcast_to(total_loss / TOTAL, (7, DIM))], axis=0)
 
     for copy in sent:
         copy.wait_send()
+
+
+def split_result(out_ref, loss_ref, mean_ref):
+    loss_ref[...] = out_ref[0, :NQ]
+    mean_ref[...] = out_ref[1, :1]
 
 
 def solution(mesh):
     row_spec = P(('replica', 'data2', 'data'))
     tok_spec = P(('replica', 'data2', 'data'), None, None)
     mask_spec = P(('replica', 'data2', 'data'), None)
-    n_msg = 12 + 12 + 32 + 16 + 4 + 3 + 3 + 7
+    n_msg = 12 + 12 + 32 + 16 + 4 + 15 + 7
 
     def local_step(query_hidden, doc_hidden, w_proj, query_mask, doc_mask, temperature):
-        losses, mean = pl.pallas_call(
+        out = pl.pallas_call(
             kernel,
-            out_shape=(jax.ShapeDtypeStruct((1, NQ), jnp.float32), jax.ShapeDtypeStruct((1, 1), jnp.float32)),
-            in_specs=[pl.BlockSpec(memory_space=pl.ANY)] * 6,
-            out_specs=(pl.BlockSpec(memory_space=pltpu.VMEM), pl.BlockSpec(memory_space=pltpu.VMEM)),
+            out_shape=jax.ShapeDtypeStruct((8, DIM), jnp.float32),
+            in_specs=[pl.BlockSpec(memory_space=pltpu.HBM)] * 6,
+            out_specs=pl.BlockSpec(memory_space=pltpu.VMEM),
             scratch_shapes=[
                 pltpu.VMEM((NQ * LQ, HID), jnp.bfloat16),
                 pltpu.VMEM((NQ, LD, HID), jnp.bfloat16),
@@ -283,17 +298,23 @@
                 pltpu.VMEM((NQ, SIDE * SIDE, SIDE * LQ, DIM), jnp.bfloat16),
                 pltpu.VMEM((2 * NQ, LD, DIM), jnp.bfloat16),
                 pltpu.VMEM((2, 8, DIM), jnp.float32),
-                pltpu.VMEM((SIDE, 8, DIM), jnp.float32),
-                pltpu.VMEM((SIDE, 8, DIM), jnp.float32),
+                pltpu.VMEM((SIDE * SIDE, 8, DIM), jnp.float32),
                 pltpu.VMEM((2 * SIDE, 8, DIM), jnp.float32),
                 pltpu.SemaphoreType.DMA((9,)),
                 pltpu.SemaphoreType.DMA((n_msg,)),
                 pltpu.SemaphoreType.DMA((n_msg,)),
             ],
-            compiler_params=pltpu.CompilerParams(collective_id=0, has_side_effects=True, vmem_limit_bytes=48 << 20),
+            compiler_params=pltpu.CompilerParams(collective_id=0, has_side_effects=True, vmem_limit_bytes=67043328),
             name='late_interaction_loss',
         )(query_hidden.reshape(NQ * LQ, HID), doc_hidden, w_proj, query_mask, doc_mask, temperature.reshape(1))
-        return losses.reshape(NQ), mean.reshape(1)
+        losses, mean = pl.pallas_call(
+            split_result,
+            out_shape=(jax.ShapeDtypeStruct((NQ,), jnp.float32), jax.ShapeDtypeStruct((1,), jnp.float32)),
+            in_specs=[pl.BlockSpec(memory_space=pltpu.VMEM)],
+            out_specs=(pl.BlockSpec(memory_space=pltpu.VMEM), pl.BlockSpec(memory_space=pltpu.VMEM)),
+            name='split_result',
+        )(out)
+        return losses, mean
 
     return jax.shard_map(local_step, mesh=mesh, in_specs=(tok_spec, tok_spec, P(None, None), mask_spec, mask_spec, P()),
                          out_specs=(row_spec, P('replica')), check_vma=False)

time: 59.3 us -> 49.6 us (0.84)
  local copies, waits for them, and re-layouts: 5.63 us -> 0 us
  Pallas kernels: 50.4 us -> 48.1 us
  between operations: 2.99 us -> 1.29 us
    unnamed x11 -> x0, local copies, waits for them, and re-layouts: 5.63 us -> none
    pallas_call x1 -> x2, Pallas kernels: 50.4 us -> 48.1 us  [the longest x1 46.9 us: local_step(): pl.pallas_call(kernel, out_shape=jax.ShapeDtypeStruct((8, DIM), jnp.float...]
where the time goes in v2:
time: 49.6 us; the launch traced here: 49.4 us
  Pallas kernels  48.1 us (97%)
  between operations  1.29 us (3%)
    pallas_call x1, Pallas kernels, local_step(): pl.pallas_call(kernel, out_shape=jax.ShapeDtypeStruct((8, DIM), jnp.float...  46.9 us
    pallas_call x1, Pallas kernels, local_step(): pl.pallas_call(split_result, out_shape=(jax.ShapeDtypeStruct((NQ,), jnp.f...  1.2 us

profile of v2, /device:TPU:1, one launch (start us, length us, event | category | flops | bytes accessed | tf_op | source)
XLA Modules:
  0.0 49.4 jit_solution(987944819468825122)
XLA Ops:
  1.3 46.9 %late_interaction_loss.1.out_ref = f32[8,128]{1,0:T(8,128)} custom-call(bf16[128,768]{1,0:T(8,128)(2,1)} %bitcast.3, bf16[4,512,768]{2,1,0:T(8,128)(2,1)} %dh_hbm.1, bf16[768,128]{1,0:T(8,128)(2,1)} %w_hbm.1, s32[4,32]{1,0:T(4,128)} %qm_hbm.1, s32[4,512]{1,0:T(4,128)} %dm_hbm.1, f32[1]{0:T(128)} %bitcast.2.temp_hbm), custom_call_target="tpu_custom_call" | custom-call | tf_op jit(solution)/shard_map/late_interaction_loss/pallas_call | solution.py:286
  48.2 1.2 %split_result.1 = (f32[4]{0:T(128)}, f32[1]{0:T(128)}) custom-call(f32[8,128]{1,0:T(8,128)} %late_interaction_loss.1.out_ref), custom_call_target="tpu_custom_call" | custom-call | tf_op jit(solution)/shard_map/split_result/pallas_call | solution.py:310

commit v3 on v2

--- a/solution.py
+++ b/solution.py
@@ -11,7 +11,7 @@
 NQ, LQ, LD, HID, DIM = 4, 32, 512, 768, 128
 SIDE = 4
 TOTAL = 512
-ORDERS = (('x', 'y', 'z'), ('y', 'z', 'x'), ('z', 'x', 'y'), ('x', 'z', 'y'))
+ORDERS = (('x', 'y', 'z'), ('y', 'z', 'x'), ('z', 'x', 'y'), ('z', 'y', 'x'))
 
 
 def unit_rows(projected):
@@ -176,35 +176,23 @@
         if forward:
             push(m4[o, r], row(o, -s, r), row(o, -s, r), moved(ORDERS[o][2], s))
 
-    for o in range(NQ):
-        second(o, 1)
-        second(o, 3)
+    def each(fn, *calls):
+        for call in calls:
+            for o in range(NQ):
+                fn(o, *call)
+
+    def last(o, r):
+        arrived(m4[o, r], row(o, 2, r))
+
+    each(second, (1,), (3,))
     score(rows((0, 1), (0, 3)))
-    for o in range(NQ):
-        third(o, 1, 0, True)
-        third(o, 3, 0, False)
-    for o in range(NQ):
-        second(o, 2)
-    score(rows((1, 0), (3, 0)))
-    for o in range(NQ):
-        third(o, 1, 1, True)
-        third(o, 3, 3, True)
-    for o in range(NQ):
-        third(o, 1, 3, False)
-        third(o, 3, 1, False)
-    score(rows((0, 2), (1, 1)))
-    for o in range(NQ):
-        third(o, 3, 2, True)
-        third(o, 1, 2, False)
-    score(rows((1, 3), (3, 1), (3, 3), (1, 2)))
-    for o in range(NQ):
-        arrived(m4[o, 0], row(o, 2, 0))
-        arrived(m4[o, 1], row(o, 2, 1))
-        arrived(m4[o, 3], row(o, 2, 3))
-    score(rows((3, 2), (2, 0), (2, 1), (2, 3)))
-    for o in range(NQ):
-        arrived(m4[o, 2], row(o, 2, 2))
-    score(rows((2, 2)))
+    each(third, (1, 0, True), (3, 0, False))
+    each(second, (2,))
+    score(rows((1, 0), (3, 0), (0, 2)))
+    each(third, (1, 1, True), (3, 3, True), (3, 2, True), (1, 3, False), (3, 1, False), (1, 2, False))
+    score(rows((1, 1), (1, 3), (3, 1), (3, 3), (1, 2), (3, 2)))
+    each(last, (0,), (1,), (3,), (2,))
+    score(rows((2, 0), (2, 1), (2, 3), (2, 2)))
 
     loads[4].wait()
     lane1 = lane[:1]
@@ -234,9 +222,13 @@
 
     at = here['y'] * SIDE + here['x']
     xybuf[at] = part
+    gathered = list(sent)
+    sent.clear()
     plane = [(sx, sy) for sy in (2, 1, 3, 0) for sx in (2, 1, 3, 0) if sx or sy]
     for sx, sy in plane:
         push(mxy[sx, sy], xybuf.at[at], xybuf.at[at], moved('x', sx, True, 'y', sy))
+    for copy in gathered:
+        copy.wait_send()
     for sx, sy in plane[::-1]:
         arrived(mxy[sx, sy], xybuf.at[((here['y'] - sy) % SIDE) * SIDE + (here['x'] - sx) % SIDE])
     part = jnp.concatenate([*merge([xybuf[i] for i in range(SIDE * SIDE)]), jnp.zeros((2, DIM), jnp.float32)], axis=0)

time: 49.6 us -> 48.4 us (0.976)
  Pallas kernels: 48.1 us -> 46.9 us
    pallas_call x1, Pallas kernels: 46.9 us -> 45.7 us  [local_step(): pl.pallas_call(kernel, out_shape=jax.ShapeDtypeStruct((8, DIM), jnp.float...]
where the time goes in v3:
time: 48.4 us; the launch traced here: 48.2 us
  Pallas kernels  46.9 us (97%)
  between operations  1.29 us (3%)
    pallas_call x1, Pallas kernels, local_step(): pl.pallas_call(kernel, out_shape=jax.ShapeDtypeStruct((8, DIM), jnp.float...  45.7 us
    pallas_call x1, Pallas kernels, local_step(): pl.pallas_call(split_result, out_shape=(jax.ShapeDtypeStruct((NQ,), jnp.f...  1.2 us

profile of v3, /device:TPU:1, one launch (start us, length us, event | category | flops | bytes accessed | tf_op | source)
XLA Modules:
  0.0 48.2 jit_solution(9306864972361983882)
XLA Ops:
  1.3 45.7 %late_interaction_loss.1.out_ref = f32[8,128]{1,0:T(8,128)} custom-call(bf16[128,768]{1,0:T(8,128)(2,1)} %bitcast.3, bf16[4,512,768]{2,1,0:T(8,128)(2,1)} %dh_hbm.1, bf16[768,128]{1,0:T(8,128)(2,1)} %w_hbm.1, s32[4,32]{1,0:T(4,128)} %qm_hbm.1, s32[4,512]{1,0:T(4,128)} %dm_hbm.1, f32[1]{0:T(128)} %bitcast.2.temp_hbm), custom_call_target="tpu_custom_call" | custom-call | tf_op jit(solution)/shard_map/late_interaction_loss/pallas_call | solution.py:278
  47.0 1.2 %split_result.1 = (f32[4]{0:T(128)}, f32[1]{0:T(128)}) custom-call(f32[8,128]{1,0:T(8,128)} %late_interaction_loss.1.out_ref), custom_call_target="tpu_custom_call" | custom-call | tf_op jit(solution)/shard_map/split_result/pallas_call | solution.py:302

commit v4 on v3

--- a/solution.py
+++ b/solution.py
@@ -161,10 +161,10 @@
             push(m3[o, s, 0], row(o, 0, 0), row(o, 0, 0), moved(ORDERS[o][2], s))
     for d in range(NQ):
         arrived(mp[d], pbuf.at[NQ + d])
+    for o in range(NQ):
+        push(m2[o, 2], row(o, 0, 0), row(o, 0, 0), moved(ORDERS[o][1], 2))
+
     score(rows((0, 0)))
-    for o in range(NQ):
-        push(m2[o, 2], row(o, 0, 0), row(o, 0, 0), moved(ORDERS[o][1], 2))
-
     def second(o, s):
         r = -s % SIDE
         arrived(m2[o, s], row(o, 0, r))
@@ -186,8 +186,8 @@
 
     each(second, (1,), (3,))
     score(rows((0, 1), (0, 3)))
+    each(second, (2,))
     each(third, (1, 0, True), (3, 0, False))
-    each(second, (2,))
     score(rows((1, 0), (3, 0), (0, 2)))
     each(third, (1, 1, True), (3, 3, True), (3, 2, True), (1, 3, False), (3, 1, False), (1, 2, False))
     score(rows((1, 1), (1, 3), (3, 1), (3, 3), (1, 2), (3, 2)))

time: 48.4 us -> 48.2 us (level)
  no operation moved by 1% of the time
where the time goes in v4:
time: 48.2 us; the launch traced here: 48 us
  Pallas kernels  46.7 us (97%)
  between operations  1.29 us (3%)
    pallas_call x1, Pallas kernels, local_step(): pl.pallas_call(kernel, out_shape=jax.ShapeDtypeStruct((8, DIM), jnp.float...  45.5 us
    pallas_call x1, Pallas kernels, local_step(): pl.pallas_call(split_result, out_shape=(jax.ShapeDtypeStruct((NQ,), jnp.f...  1.2 us

profile of v4, /device:TPU:1, one launch (start us, length us, event | category | flops | bytes accessed | tf_op | source)
XLA Modules:
  0.0 48.0 jit_solution(1496226702876570184)
XLA Ops:
  1.3 45.5 %late_interaction_loss.1.out_ref = f32[8,128]{1,0:T(8,128)} custom-call(bf16[128,768]{1,0:T(8,128)(2,1)} %bitcast.3, bf16[4,512,768]{2,1,0:T(8,128)(2,1)} %dh_hbm.1, bf16[768,128]{1,0:T(8,128)(2,1)} %w_hbm.1, s32[4,32]{1,0:T(4,128)} %qm_hbm.1, s32[4,512]{1,0:T(4,128)} %dm_hbm.1, f32[1]{0:T(128)} %bitcast.2.temp_hbm), custom_call_target="tpu_custom_call" | custom-call | tf_op jit(solution)/shard_map/late_interaction_loss/pallas_call | solution.py:278
  46.8 1.2 %split_result.1 = (f32[4]{0:T(128)}, f32[1]{0:T(128)}) custom-call(f32[8,128]{1,0:T(8,128)} %late_interaction_loss.1.out_ref), custom_call_target="tpu_custom_call" | custom-call | tf_op jit(solution)/shard_map/split_result/pallas_call | solution.py:302
